TPU v7x, 32 devices: a whole 2x2x4 slice. The times are simulated.
32 devices in a mesh: grp: 4 (over y, x), dev: 8 (over z, core).
Axes of the slice: x: 2, y: 2, z: 4, core: 2. Of those that a mesh axis runs over, the one named last changes fastest.
Arguments:
- examples: float32 [2048, 32768], P(('grp', 'dev'))
- labels: int32 [2048], P(('grp', 'dev')), may hold values from 0 to 1, as said below
Outputs:
- consensus: float32 [32768], replicated
- local_weights: float32 [32, 32768], P(('grp', 'dev'))
- dual_vars: float32 [32, 32768], P(('grp', 'dev'))
Inputs may be any that keep to these rules, and one draw needn't show every extreme that they name: `labels`: each example's class, 0 or 1.
All inputs are finite; a program needn't handle non-finite values.
Results may differ from a plain program's by a relative error of at most 0.00012.
Values sent between devices are 32-bit elements; how exact they have to be, the bound alone decides.
A program may use at most 64 MiB of HBM per device.

v0:
```python
import jax
import jax.numpy as jnp
from jax import lax
from jax.sharding import PartitionSpec as P

PROX = 3
ROUNDS = 4
step_size = 200.0
penalty = 0.005
thresh = 0.04


def shrink(values):
    return values - jnp.clip(values, -thresh, thresh)


def local_steps(examples, targets, weight_vector, consensus_point):
    for prox_index in range(PROX):
        label_margins = jnp.dot(examples, weight_vector, precision=lax.Precision.HIGHEST)
        primal_residual = jax.nn.sigmoid(label_margins) - targets
        loss_gradient = jnp.dot(primal_residual, examples, precision=lax.Precision.HIGHEST)
        weight_vector = (
            weight_vector - step_size * loss_gradient + step_size * penalty * consensus_point
        ) / (1.0 + step_size * penalty)
    return weight_vector


def per_device(examples, labels):
    members = lax.axis_size("grp") * lax.axis_size("dev")
    targets = labels.astype(jnp.float32)
    width = examples.shape[1]

    def one_round(round_index, carried):
        consensus, weight_vector, dual_vars = carried
        consensus_point = consensus - dual_vars
        weight_vector = local_steps(examples, targets, weight_vector, consensus_point)
        combined = weight_vector + dual_vars
        summed = lax.psum(combined, ("grp", "dev"))
        consensus = shrink(summed / members)
        dual_vars = dual_vars + weight_vector - consensus
        return (consensus, weight_vector, dual_vars)

    start = (
        jnp.zeros((width,), jnp.float32),
        jnp.zeros((width,), jnp.float32),
        jnp.zeros((width,), jnp.float32),
    )
    consensus, weight_vector, dual_vars = lax.fori_loop(0, ROUNDS, one_round, start)
    return (consensus, weight_vector[None, :], dual_vars[None, :])


def solution(mesh):
    placed = (P(("grp", "dev"), None), P(("grp", "dev")))
    return jax.shard_map(
        per_device,
        mesh=mesh,
        in_specs=placed,
        out_specs=(P(), P(("grp", "dev"), None), P(("grp", "dev"), None)),
        check_vma=False,
    )
```

profile of v0, /device:TPU:0, one launch (start us, length us, event | category | flops | bytes accessed | tf_op | source)
XLA Modules:
  0.0 658.6 jit_solution(14624794344501646285)
XLA Ops:
  7.2 0.7 convert_element_type.3
  7.8 643.4 %while.15 = (s32[]{:T(128)}, f32[32768]{0:T(1024)S(1)}, f32[32768]{0:T(1024)S(1)}, f32[32768]{0:T(1024)S(1)}, f32[64,32768]{1,0:T(8,128)}, /*index=5*/f32[64]{0:T(128)S(1)}, s32[]{:T(128)}, s32[]{:T(128)}) while((s32[]{:T(128)}, f32[32768]{0:T(1024)S(1)}, f32[32768]{0:T(1024)S(1)}, f32[32768]{0:T(1024)S(1)}, ...), condition=%wide.region_2.3_spmd.clone, body=%wide.region_0.2_spmd.clone.sunk | while | flops 151782144 | bytes 88344992 | solution.py:48
  7.8 0.0 all-reduce.2.cloned.1.call-start
  7.8 0.0 copy-start
  7.9 9.1 %fusion.65 = f32[64,1]{0,1:T(1,128)S(1)} fusion(f32[64]{0:T(128)S(1)} %get-tuple-element.149, f32[64,32768]{1,0:T(8,128)} %get-tuple-element.148, f32[32768,1]{0,1:T(1,128)S(1)} %bitcast.118), kind=kOutput, calls=%fused_computation.20.clone.1 | convolution fusion | flops 25166080 | bytes 8520192 | tf_op jit(solution)/shard_map/while/body/eval_jaxpr/dot_general | solution.py:19
  16.9 0.0 copy-done
  16.9 4.0 fusion.66
  21.0 6.6 fusion.67
  27.6 4.1 fusion.68
  31.7 6.6 fusion.69
  38.3 4.1 fusion.70
  42.3 0.7 select_add_fusion.2
  43.0 0.0 all-reduce.2.cloned.1.call-update
  43.0 127.3 %all-reduce.2.cloned.1.call-done = f32[32768]{0:T(1024)} async-done(((f32[32768]{0:T(1024)}), f32[32768]{0:T(1024)}) %all-reduce.2.cloned.1.call-update) | async-done | bytes 131088 | tf_op jit(solution)/shard_map/while/body/eval_jaxpr/psum | solution.py:38
  170.4 1.0 fusion.71
  171.4 0.0 all-reduce.2.cloned.1.call-start
  171.4 0.0 copy-start
  171.5 9.1 %fusion.65 = f32[64,1]{0,1:T(1,128)S(1)} fusion(f32[64]{0:T(128)S(1)} %get-tuple-element.149, f32[64,32768]{1,0:T(8,128)} %get-tuple-element.148, f32[32768,1]{0,1:T(1,128)S(1)} %bitcast.118), kind=kOutput, calls=%fused_computation.20.clone.1 | convolution fusion | flops 25166080 | bytes 8520192 | tf_op jit(solution)/shard_map/while/body/eval_jaxpr/dot_general | solution.py:19
  180.5 0.0 copy-done
  180.5 4.0 fusion.66
  184.6 6.6 fusion.67
  191.2 4.1 fusion.68
  195.3 6.6 fusion.69
  201.9 4.1 fusion.70
  205.9 0.7 select_add_fusion.2
  206.6 0.0 all-reduce.2.cloned.1.call-update
  206.6 123.7 %all-reduce.2.cloned.1.call-done = f32[32768]{0:T(1024)} async-done(((f32[32768]{0:T(1024)}), f32[32768]{0:T(1024)}) %all-reduce.2.cloned.1.call-update) | async-done | bytes 131088 | tf_op jit(solution)/shard_map/while/body/eval_jaxpr/psum | solution.py:38
  330.3 1.0 fusion.71
  331.3 0.0 all-reduce.2.cloned.1.call-start
  331.4 0.0 copy-start
  331.4 9.1 %fusion.65 = f32[64,1]{0,1:T(1,128)S(1)} fusion(f32[64]{0:T(128)S(1)} %get-tuple-element.149, f32[64,32768]{1,0:T(8,128)} %get-tuple-element.148, f32[32768,1]{0,1:T(1,128)S(1)} %bitcast.118), kind=kOutput, calls=%fused_computation.20.clone.1 | convolution fusion | flops 25166080 | bytes 8520192 | tf_op jit(solution)/shard_map/while/body/eval_jaxpr/dot_general | solution.py:19
  340.5 0.0 copy-done
  340.5 4.0 fusion.66
  344.6 6.6 fusion.67
  351.2 4.1 fusion.68
  355.3 6.6 fusion.69
  361.8 4.1 fusion.70
  365.9 0.7 select_add_fusion.2
  366.6 0.0 all-reduce.2.cloned.1.call-update
  366.6 123.7 %all-reduce.2.cloned.1.call-done = f32[32768]{0:T(1024)} async-done(((f32[32768]{0:T(1024)}), f32[32768]{0:T(1024)}) %all-reduce.2.cloned.1.call-update) | async-done | bytes 131088 | tf_op jit(solution)/shard_map/while/body/eval_jaxpr/psum | solution.py:38
  490.3 1.0 fusion.71
  491.3 0.0 all-reduce.2.cloned.1.call-start
  491.4 0.0 copy-start
  491.4 9.1 %fusion.65 = f32[64,1]{0,1:T(1,128)S(1)} fusion(f32[64]{0:T(128)S(1)} %get-tuple-element.149, f32[64,32768]{1,0:T(8,128)} %get-tuple-element.148, f32[32768,1]{0,1:T(1,128)S(1)} %bitcast.118), kind=kOutput, calls=%fused_computation.20.clone.1 | convolution fusion | flops 25166080 | bytes 8520192 | tf_op jit(solution)/shard_map/while/body/eval_jaxpr/dot_general | solution.py:19
  500.5 0.0 copy-done
  500.5 4.0 fusion.66
  504.6 6.6 fusion.67
  511.1 4.1 fusion.68
  515.2 6.6 fusion.69
  521.8 4.1 fusion.70
  525.9 0.7 select_add_fusion.2
  526.6 0.0 all-reduce.2.cloned.1.call-update
  526.6 123.7 %all-reduce.2.cloned.1.call-done = f32[32768]{0:T(1024)} async-done(((f32[32768]{0:T(1024)}), f32[32768]{0:T(1024)}) %all-reduce.2.cloned.1.call-update) | async-done | bytes 131088 | tf_op jit(solution)/shard_map/while/body/eval_jaxpr/psum | solution.py:38
  650.3 1.0 fusion.71
  651.3 0.0 copy-start.1
  651.3 0.0 copy-start.2
  651.3 0.0 copy-start.3
  651.3 0.6 copy-done.1
  651.9 0.0 copy-done.2
  652.0 0.0 copy-done.3
  (15 shorter events, 0.4 us)
Async XLA Ops:
  7.8 162.5 %all-reduce.2.cloned.1.call-start = ((), (), s32[]{:S(2)}) async-start(), calls=%async_computation | async-start | bytes 262144 | tf_op jit(solution)/shard_map/while/body/eval_jaxpr/psum | solution.py:38
  7.8 9.1 %copy-start = (f32[64,32768]{1,0:T(8,128)S(1)}, f32[64,32768]{1,0:T(8,128)}, u32[]{:S(2)}) copy-start(f32[64,32768]{1,0:T(8,128)} %get-tuple-element.148) | copy-start | bytes 25165828 | tf_op jit(solution)/shard_map/while
  171.4 159.0 %all-reduce.2.cloned.1.call-start = ((), (), s32[]{:S(2)}) async-start(), calls=%async_computation | async-start | bytes 262144 | tf_op jit(solution)/shard_map/while/body/eval_jaxpr/psum | solution.py:38
  171.4 9.1 %copy-start = (f32[64,32768]{1,0:T(8,128)S(1)}, f32[64,32768]{1,0:T(8,128)}, u32[]{:S(2)}) copy-start(f32[64,32768]{1,0:T(8,128)} %get-tuple-element.148) | copy-start | bytes 25165828 | tf_op jit(solution)/shard_map/while
  331.3 159.0 %all-reduce.2.cloned.1.call-start = ((), (), s32[]{:S(2)}) async-start(), calls=%async_computation | async-start | bytes 262144 | tf_op jit(solution)/shard_map/while/body/eval_jaxpr/psum | solution.py:38
  331.4 9.1 %copy-start = (f32[64,32768]{1,0:T(8,128)S(1)}, f32[64,32768]{1,0:T(8,128)}, u32[]{:S(2)}) copy-start(f32[64,32768]{1,0:T(8,128)} %get-tuple-element.148) | copy-start | bytes 25165828 | tf_op jit(solution)/shard_map/while
  491.3 159.0 %all-reduce.2.cloned.1.call-start = ((), (), s32[]{:S(2)}) async-start(), calls=%async_computation | async-start | bytes 262144 | tf_op jit(solution)/shard_map/while/body/eval_jaxpr/psum | solution.py:38
  491.4 9.1 %copy-start = (f32[64,32768]{1,0:T(8,128)S(1)}, f32[64,32768]{1,0:T(8,128)}, u32[]{:S(2)}) copy-start(f32[64,32768]{1,0:T(8,128)} %get-tuple-element.148) | copy-start | bytes 25165828 | tf_op jit(solution)/shard_map/while
  651.3 0.7 copy-start.1
  651.3 0.7 copy-start.2
  651.3 0.7 copy-start.3
Sparse Core Ops, SparseCore 0:
  43.2 127.1 all-reduce.1
  206.8 123.5 all-reduce.1
  366.7 123.5 all-reduce.1
  526.7 123.5 all-reduce.1
where the time goes:
time: 659 us
  waiting for transfers between devices  498 us (76%)
  matrix products  137 us (21%)
  between operations  13.7 us (2%)
  other arithmetic  7.74 us (1%)
    psum x4, waiting for transfers between devices, one_round(): summed = lax.psum(combined, ('grp', 'dev'))  498 us
    dot_general x12, matrix products, local_steps(): jnp.dot(examples, weight_vector, precision=lax.Precision.HIGHEST)  88.9 us
    dot_general x12, matrix products, local_steps(): jnp.dot(primal_residual, examples, precision=lax.Precision.HIGHEST)  48.6 us
  transfers between devices with their start and end apart: 4, of which 4 were waited for; matrix products, arithmetic and copies ran while one was open for 0% of the time, Pallas kernels for 0%

commit v1 on v0

--- a/solution.py
+++ b/solution.py
@@ -35,7 +35,7 @@
         consensus_point = consensus - dual_vars
         weight_vector = local_steps(examples, targets, weight_vector, consensus_point)
         combined = weight_vector + dual_vars
-        summed = lax.psum(combined, ("grp", "dev"))
+        summed = jnp.sum(lax.all_gather(combined, ("grp", "dev")), axis=0)
         consensus = shrink(summed / members)
         dual_vars = dual_vars + weight_vector - consensus
         return (consensus, weight_vector, dual_vars)

time: 659 us -> 434 us (0.66)
  waiting for transfers between devices: 498 us -> 246 us
  local copies, waits for them, and re-layouts: 0.75 us -> 20.6 us
    psum x4 -> x0, waiting for transfers between devices: 498 us -> none  [one_round(): summed = lax.psum(combined, ('grp', 'dev'))]
    all_gather x0 -> x4, waiting for transfers between devices: none -> 246 us  [one_round(): summed = jnp.sum(lax.all_gather(combined, ('grp', 'dev')), axis=0)]
    all_gather x0 -> x4, local copies, waits for them, and re-layouts: none -> 19.9 us  [one_round(): summed = jnp.sum(lax.all_gather(combined, ('grp', 'dev')), axis=0)]
    reduce_sum x0 -> x4, other arithmetic: none -> 10.4 us  [one_round(): summed = jnp.sum(lax.all_gather(combined, ('grp', 'dev')), axis=0)]
where the time goes in v1:
time: 434 us; the launch traced here: 433 us
  waiting for transfers between devices  246 us (57%)
  matrix products  137 us (32%)
  local copies, waits for them, and re-layouts  20.6 us (5%)
  other arithmetic  14.3 us (3%)
  between operations  13.7 us (3%)
    all_gather x4, waiting for transfers between devices, one_round(): summed = jnp.sum(lax.all_gather(combined, ('grp', 'dev')), axis=0)  246 us
    dot_general x12, matrix products, local_steps(): jnp.dot(examples, weight_vector, precision=lax.Precision.HIGHEST)  88.9 us
    dot_general x12, matrix products, local_steps(): jnp.dot(primal_residual, examples, precision=lax.Precision.HIGHEST)  48.6 us
    all_gather x4, local copies, waits for them, and re-layouts, one_round(): summed = jnp.sum(lax.all_gather(combined, ('grp', 'dev')), axis=0)  19.9 us
    reduce_sum x4, other arithmetic, one_round(): summed = jnp.sum(lax.all_gather(combined, ('grp', 'dev')), axis=0)  10.4 us
  transfers between devices with their start and end apart: 4, of which 4 were waited for; matrix products, arithmetic and copies ran while one was open for 0% of the time, Pallas kernels for 0%

profile of v1, /device:TPU:0, one launch (start us, length us, event | category | flops | bytes accessed | tf_op | source)
XLA Modules:
  0.0 433.0 jit_solution(9894575466883503148)
XLA Ops:
  7.2 0.7 convert_element_type.3
  7.8 417.9 %while.15 = (s32[]{:T(128)}, f32[32768]{0:T(1024)S(1)}, f32[32768]{0:T(1024)S(1)}, f32[32768]{0:T(1024)S(1)}, f32[64,32768]{1,0:T(8,128)}, /*index=5*/f32[64]{0:T(128)S(1)}, s32[]{:T(128)}, s32[]{:T(128)}, f32[]{:T(128)}) while((s32[]{:T(128)}, f32[32768]{0:T(1024)S(1)}, f32[32768]{0:T(1024)S(1)}, f32[32768]{0:T(1024)S(1)}, ...), condition=%wide.region_2.3_spmd.clone, body=%wide.region_0.2_spmd.clone.sunk | while | flops 152765184 | bytes 113772992 | solution.py:48
  7.8 0.0 all-gather.6.cloned.1.call-start
  7.9 9.1 %fusion.65 = f32[64,1]{0,1:T(1,128)S(1)} fusion(f32[64]{0:T(128)S(1)} %get-tuple-element.151, f32[64,32768]{1,0:T(8,128)} %get-tuple-element.150, f32[32768,1]{0,1:T(1,128)S(1)} %bitcast.118), kind=kOutput, calls=%fused_computation.20.clone.1 | convolution fusion | flops 25166080 | bytes 8520192 | tf_op jit(solution)/shard_map/while/body/eval_jaxpr/dot_general | solution.py:19
  16.9 0.0 copy-done
  16.9 4.0 fusion.66
  21.0 6.6 %fusion.67 = f32[64,1]{0,1:T(1,128)S(1)} fusion(f32[64]{0:T(128)S(1)} %get-tuple-element.151, f32[32768,1]{0,1:T(1,128)S(1)} %bitcast.117, f32[64,32768]{1,0:T(8,128)S(1)} %copy-done), kind=kOutput, calls=%fused_computation.13.clone.1 | convolution fusion | flops 25166080 | bytes 8520192 | tf_op jit(solution)/shard_map/while/body/eval_jaxpr/dot_general | solution.py:19
  27.6 4.1 fusion.68
  31.7 6.6 %fusion.69 = f32[64,1]{0,1:T(1,128)S(1)} fusion(f32[64]{0:T(128)S(1)} %get-tuple-element.151, f32[32768,1]{0,1:T(1,128)S(1)} %bitcast.116, f32[64,32768]{1,0:T(8,128)S(1)} %copy-done), kind=kOutput, calls=%fused_computation.6.clone.1 | convolution fusion | flops 25166080 | bytes 8520192 | tf_op jit(solution)/shard_map/while/body/eval_jaxpr/dot_general | solution.py:19
  38.3 4.1 fusion.70
  42.3 0.7 select_add_fusion.2
  43.0 0.0 all-gather.6.cloned.1.call-update
  43.0 64.5 %all-gather.6.cloned.1.call-done = f32[1048576]{0:T(1024)} async-done(((f32[32768]{0:T(1024)}), f32[1048576]{0:T(1024)}) %all-gather.6.cloned.1.call-update) | async-done | bytes 4194320 | tf_op jit(solution)/shard_map/while/body/eval_jaxpr/all_gather | solution.py:38
  107.6 5.0 %reshape.21 = f32[32,32768]{1,0:T(8,128)} reshape(f32[1048576]{0:T(1024)} %all-gather.6.cloned.1.call-done) | data formatting | bytes 8388608 | tf_op jit(solution)/shard_map/while/body/eval_jaxpr/all_gather | solution.py:38
  112.6 2.6 reduce_sum.11
  115.2 0.0 all-gather.6.cloned.1.call-start
  115.3 0.0 copy-start
  115.3 9.1 %fusion.65 = f32[64,1]{0,1:T(1,128)S(1)} fusion(f32[64]{0:T(128)S(1)} %get-tuple-element.151, f32[64,32768]{1,0:T(8,128)} %get-tuple-element.150, f32[32768,1]{0,1:T(1,128)S(1)} %bitcast.118), kind=kOutput, calls=%fused_computation.20.clone.1 | convolution fusion | flops 25166080 | bytes 8520192 | tf_op jit(solution)/shard_map/while/body/eval_jaxpr/dot_general | solution.py:19
  124.4 0.0 copy-done
  124.4 4.0 fusion.66
  128.5 6.6 %fusion.67 = f32[64,1]{0,1:T(1,128)S(1)} fusion(f32[64]{0:T(128)S(1)} %get-tuple-element.151, f32[32768,1]{0,1:T(1,128)S(1)} %bitcast.117, f32[64,32768]{1,0:T(8,128)S(1)} %copy-done), kind=kOutput, calls=%fused_computation.13.clone.1 | convolution fusion | flops 25166080 | bytes 8520192 | tf_op jit(solution)/shard_map/while/body/eval_jaxpr/dot_general | solution.py:19
  135.1 4.1 fusion.68
  139.1 6.6 %fusion.69 = f32[64,1]{0,1:T(1,128)S(1)} fusion(f32[64]{0:T(128)S(1)} %get-tuple-element.151, f32[32768,1]{0,1:T(1,128)S(1)} %bitcast.116, f32[64,32768]{1,0:T(8,128)S(1)} %copy-done), kind=kOutput, calls=%fused_computation.6.clone.1 | convolution fusion | flops 25166080 | bytes 8520192 | tf_op jit(solution)/shard_map/while/body/eval_jaxpr/dot_general | solution.py:19
  145.7 4.1 fusion.70
  149.8 0.7 select_add_fusion.2
  150.5 0.0 all-gather.6.cloned.1.call-update
  150.5 60.6 %all-gather.6.cloned.1.call-done = f32[1048576]{0:T(1024)} async-done(((f32[32768]{0:T(1024)}), f32[1048576]{0:T(1024)}) %all-gather.6.cloned.1.call-update) | async-done | bytes 4194320 | tf_op jit(solution)/shard_map/while/body/eval_jaxpr/all_gather | solution.py:38
  211.1 5.0 %reshape.21 = f32[32,32768]{1,0:T(8,128)} reshape(f32[1048576]{0:T(1024)} %all-gather.6.cloned.1.call-done) | data formatting | bytes 8388608 | tf_op jit(solution)/shard_map/while/body/eval_jaxpr/all_gather | solution.py:38
  216.1 2.6 reduce_sum.11
  218.7 0.0 copy-done.1
  218.7 0.0 all-gather.6.cloned.1.call-start
  218.8 0.0 copy-start
  218.8 9.1 %fusion.65 = f32[64,1]{0,1:T(1,128)S(1)} fusion(f32[64]{0:T(128)S(1)} %get-tuple-element.151, f32[64,32768]{1,0:T(8,128)} %get-tuple-element.150, f32[32768,1]{0,1:T(1,128)S(1)} %bitcast.118), kind=kOutput, calls=%fused_computation.20.clone.1 | convolution fusion | flops 25166080 | bytes 8520192 | tf_op jit(solution)/shard_map/while/body/eval_jaxpr/dot_general | solution.py:19
  227.9 0.0 copy-done
  227.9 4.0 fusion.66
  232.0 6.6 %fusion.67 = f32[64,1]{0,1:T(1,128)S(1)} fusion(f32[64]{0:T(128)S(1)} %get-tuple-element.151, f32[32768,1]{0,1:T(1,128)S(1)} %bitcast.117, f32[64,32768]{1,0:T(8,128)S(1)} %copy-done), kind=kOutput, calls=%fused_computation.13.clone.1 | convolution fusion | flops 25166080 | bytes 8520192 | tf_op jit(solution)/shard_map/while/body/eval_jaxpr/dot_general | solution.py:19
  238.6 4.1 fusion.68
  242.7 6.6 %fusion.69 = f32[64,1]{0,1:T(1,128)S(1)} fusion(f32[64]{0:T(128)S(1)} %get-tuple-element.151, f32[32768,1]{0,1:T(1,128)S(1)} %bitcast.116, f32[64,32768]{1,0:T(8,128)S(1)} %copy-done), kind=kOutput, calls=%fused_computation.6.clone.1 | convolution fusion | flops 25166080 | bytes 8520192 | tf_op jit(solution)/shard_map/while/body/eval_jaxpr/dot_general | solution.py:19
  249.2 4.1 fusion.70
  253.3 0.7 select_add_fusion.2
  254.0 0.0 all-gather.6.cloned.1.call-update
  254.0 60.6 %all-gather.6.cloned.1.call-done = f32[1048576]{0:T(1024)} async-done(((f32[32768]{0:T(1024)}), f32[1048576]{0:T(1024)}) %all-gather.6.cloned.1.call-update) | async-done | bytes 4194320 | tf_op jit(solution)/shard_map/while/body/eval_jaxpr/all_gather | solution.py:38
  314.6 5.0 %reshape.21 = f32[32,32768]{1,0:T(8,128)} reshape(f32[1048576]{0:T(1024)} %all-gather.6.cloned.1.call-done) | data formatting | bytes 8388608 | tf_op jit(solution)/shard_map/while/body/eval_jaxpr/all_gather | solution.py:38
  319.6 2.6 reduce_sum.11
  322.2 0.0 all-gather.6.cloned.1.call-start
  322.3 0.0 copy-start
  322.3 9.1 %fusion.65 = f32[64,1]{0,1:T(1,128)S(1)} fusion(f32[64]{0:T(128)S(1)} %get-tuple-element.151, f32[64,32768]{1,0:T(8,128)} %get-tuple-element.150, f32[32768,1]{0,1:T(1,128)S(1)} %bitcast.118), kind=kOutput, calls=%fused_computation.20.clone.1 | convolution fusion | flops 25166080 | bytes 8520192 | tf_op jit(solution)/shard_map/while/body/eval_jaxpr/dot_general | solution.py:19
  331.4 0.0 copy-done
  331.4 4.0 fusion.66
  335.5 6.6 %fusion.67 = f32[64,1]{0,1:T(1,128)S(1)} fusion(f32[64]{0:T(128)S(1)} %get-tuple-element.151, f32[32768,1]{0,1:T(1,128)S(1)} %bitcast.117, f32[64,32768]{1,0:T(8,128)S(1)} %copy-done), kind=kOutput, calls=%fused_computation.13.clone.1 | convolution fusion | flops 25166080 | bytes 8520192 | tf_op jit(solution)/shard_map/while/body/eval_jaxpr/dot_general | solution.py:19
  342.1 4.1 fusion.68
  346.2 6.6 %fusion.69 = f32[64,1]{0,1:T(1,128)S(1)} fusion(f32[64]{0:T(128)S(1)} %get-tuple-element.151, f32[32768,1]{0,1:T(1,128)S(1)} %bitcast.116, f32[64,32768]{1,0:T(8,128)S(1)} %copy-done), kind=kOutput, calls=%fused_computation.6.clone.1 | convolution fusion | flops 25166080 | bytes 8520192 | tf_op jit(solution)/shard_map/while/body/eval_jaxpr/dot_general | solution.py:19
  352.7 4.1 fusion.70
  356.8 0.7 select_add_fusion.2
  357.5 0.0 all-gather.6.cloned.1.call-update
  357.5 60.6 %all-gather.6.cloned.1.call-done = f32[1048576]{0:T(1024)} async-done(((f32[32768]{0:T(1024)}), f32[1048576]{0:T(1024)}) %all-gather.6.cloned.1.call-update) | async-done | bytes 4194320 | tf_op jit(solution)/shard_map/while/body/eval_jaxpr/all_gather | solution.py:38
  418.1 5.0 %reshape.21 = f32[32,32768]{1,0:T(8,128)} reshape(f32[1048576]{0:T(1024)} %all-gather.6.cloned.1.call-done) | data formatting | bytes 8388608 | tf_op jit(solution)/shard_map/while/body/eval_jaxpr/all_gather | solution.py:38
  423.1 2.6 reduce_sum.11
  425.8 0.0 copy-start.2
  425.8 0.0 copy-start.3
  425.8 0.0 copy-start.4
  425.8 0.6 copy-done.2
  426.4 0.0 copy-done.3
  426.5 0.0 copy-done.4
  (27 shorter events, 0.4 us)
Async XLA Ops:
  7.8 99.8 %all-gather.6.cloned.1.call-start = ((), (), s32[]{:S(2)}) async-start(), calls=%async_computation | async-start | bytes 4325376 | tf_op jit(solution)/shard_map/while/body/eval_jaxpr/all_gather | solution.py:38
  7.8 9.1 %copy-start = (f32[64,32768]{1,0:T(8,128)S(1)}, f32[64,32768]{1,0:T(8,128)}, u32[]{:S(2)}) copy-start(f32[64,32768]{1,0:T(8,128)} %get-tuple-element.150) | copy-start | bytes 25165828 | tf_op jit(solution)/shard_map/while
  43.0 72.2 %copy-start.1 = (f32[32768]{0:T(1024)S(1)}, f32[32768]{0:T(1024)}, u32[]{:S(2)}) copy-start(f32[32768]{0:T(1024)} %get-tuple-element.124) | copy-start | bytes 393220 | tf_op jit(solution)/shard_map/while
  115.2 95.9 %all-gather.6.cloned.1.call-start = ((), (), s32[]{:S(2)}) async-start(), calls=%async_computation | async-start | bytes 4325376 | tf_op jit(solution)/shard_map/while/body/eval_jaxpr/all_gather | solution.py:38
  115.3 9.1 %copy-start = (f32[64,32768]{1,0:T(8,128)S(1)}, f32[64,32768]{1,0:T(8,128)}, u32[]{:S(2)}) copy-start(f32[64,32768]{1,0:T(8,128)} %get-tuple-element.150) | copy-start | bytes 25165828 | tf_op jit(solution)/shard_map/while
  150.5 68.2 %copy-start.1 = (f32[32768]{0:T(1024)S(1)}, f32[32768]{0:T(1024)}, u32[]{:S(2)}) copy-start(f32[32768]{0:T(1024)} %get-tuple-element.124) | copy-start | bytes 393220 | tf_op jit(solution)/shard_map/while
  218.7 95.9 %all-gather.6.cloned.1.call-start = ((), (), s32[]{:S(2)}) async-start(), calls=%async_computation | async-start | bytes 4325376 | tf_op jit(solution)/shard_map/while/body/eval_jaxpr/all_gather | solution.py:38
  218.8 9.1 %copy-start = (f32[64,32768]{1,0:T(8,128)S(1)}, f32[64,32768]{1,0:T(8,128)}, u32[]{:S(2)}) copy-start(f32[64,32768]{1,0:T(8,128)} %get-tuple-element.150) | copy-start | bytes 25165828 | tf_op jit(solution)/shard_map/while
  254.0 68.2 %copy-start.1 = (f32[32768]{0:T(1024)S(1)}, f32[32768]{0:T(1024)}, u32[]{:S(2)}) copy-start(f32[32768]{0:T(1024)} %get-tuple-element.124) | copy-start | bytes 393220 | tf_op jit(solution)/shard_map/while
  322.2 95.9 %all-gather.6.cloned.1.call-start = ((), (), s32[]{:S(2)}) async-start(), calls=%async_computation | async-start | bytes 4325376 | tf_op jit(solution)/shard_map/while/body/eval_jaxpr/all_gather | solution.py:38
  322.3 9.1 %copy-start = (f32[64,32768]{1,0:T(8,128)S(1)}, f32[64,32768]{1,0:T(8,128)}, u32[]{:S(2)}) copy-start(f32[64,32768]{1,0:T(8,128)} %get-tuple-element.150) | copy-start | bytes 25165828 | tf_op jit(solution)/shard_map/while
  357.5 68.2 %copy-start.1 = (f32[32768]{0:T(1024)S(1)}, f32[32768]{0:T(1024)}, u32[]{:S(2)}) copy-start(f32[32768]{0:T(1024)} %get-tuple-element.124) | copy-start | bytes 393220 | tf_op jit(solution)/shard_map/while
  425.8 0.7 copy-start.2
  425.8 0.7 copy-start.3
  425.8 0.7 copy-start.4
Sparse Core Ops, SparseCore 0:
  43.2 64.3 all-gather.5
  150.6 60.4 all-gather.5
  254.1 60.4 all-gather.5
  357.6 60.4 all-gather.5
